TPU v7x, 32 devices: a whole 2x2x4 slice. The times are simulated.
32 devices in a mesh: cluster: 8 (over z, y), client: 4 (over x, core).
Axes of the slice: x: 2, y: 2, z: 4, core: 2. Of those that a mesh axis runs over, the one named last changes fastest.
Arguments:
- user_feats: bfloat16 [6144, 2048], P('client'), may hold values from -6 to 6
- item_feats: bfloat16 [6144, 2048], P('client'), may hold values from -6 to 6
- item_ids: int32 [6144], P('client'), may hold values from 0 to 999
- picks: int32 [64], P('client'), may hold values from 0 to 7
- user_weight: bfloat16 [8, 2048, 512], P('cluster'), may hold values from -0.125 to 0.125
- item_weight: bfloat16 [8, 2048, 512], P('cluster'), may hold values from -0.125 to 0.125
Outputs:
- loss_table: float32 [64, 8], P('client')
- user_grad: float32 [8, 2048, 512], P('cluster', 'client')
- item_grad: float32 [8, 2048, 512], P('cluster', 'client')
Inputs may be any that keep to these rules, and one draw needn't show every extreme that they name: `picks`: one cluster per client.
All inputs are finite; a program needn't handle non-finite values.
Results may differ from a plain program's by a relative error of at most 0.005.
Values sent between devices are 32-bit elements; how exact they have to be, the bound alone decides.
No kernel may reach another device: no remote copies, remote signals or barrier semaphores. Data moves between devices by JAX's collectives and lax.ppermute only.
A program may use at most 128 MiB of HBM per device.

v0:
```python
import math

import jax
import jax.numpy as jnp
from jax import lax
from jax.sharding import PartitionSpec as P


def silu_slope(pre_act):
    sig = jax.nn.sigmoid(pre_act)
    return sig * (1.0 + pre_act * (1.0 - sig))


def contract_rows(left, right):
    return lax.dot_general(
        left, right, (((0,), (0,)), ((), ())), preferred_element_type=jnp.float32
    )


def body(user_feats, item_feats, item_ids, picks, user_weight, item_weight):
    cluster_index = lax.axis_index("cluster")
    user_map = user_weight[0]
    item_map = item_weight[0]
    clients = picks.shape[0]
    row_count = user_feats.shape[0]
    per_client = row_count // clients
    width = user_map.shape[1]
    temper = 1.0 / math.sqrt(width)
    pre_user = jnp.dot(user_feats, user_map, preferred_element_type=jnp.float32)
    user_vec = jax.nn.silu(pre_user).astype(jnp.bfloat16)
    item_vec = jnp.dot(item_feats, item_map, preferred_element_type=jnp.float32).astype(
        jnp.bfloat16
    )
    user_blocks = user_vec.reshape(clients, per_client, width)
    item_blocks = item_vec.reshape(clients, per_client, width)
    scores = (
        jnp.einsum("cre,cte->crt", user_blocks, item_blocks, preferred_element_type=jnp.float32)
        * temper
    )
    grouped = item_ids.reshape(clients, per_client)
    labels = (grouped[:, :, None] == grouped[:, None, :]).astype(jnp.float32)
    pair_loss = jax.nn.softplus(scores) - labels * scores
    client_loss = jnp.mean(pair_loss, axis=(1, 2))
    loss_table = lax.all_gather(client_loss[:, None], "cluster", axis=1, tiled=True)
    chosen = (picks == cluster_index).astype(jnp.float32)
    slope = ((jax.nn.sigmoid(scores) - labels) * temper * chosen[:, None, None]).astype(
        jnp.bfloat16
    )
    user_slope = jnp.einsum(
        "crt,cte->cre", slope, item_blocks, preferred_element_type=jnp.float32
    ).reshape(row_count, width)
    pre_slope = (user_slope * silu_slope(pre_user)).astype(jnp.bfloat16)
    item_slope = (
        jnp.einsum("crt,cre->cte", slope, user_blocks, preferred_element_type=jnp.float32)
        .reshape(row_count, width)
        .astype(jnp.bfloat16)
    )
    partial_sum = lax.psum_scatter(
        jnp.concatenate(
            [contract_rows(user_feats, pre_slope), contract_rows(item_feats, item_slope)], axis=1
        ),
        "client",
        scatter_dimension=0,
        tiled=True,
    )
    return (loss_table, partial_sum[None, :, :width], partial_sum[None, :, width:])


def solution(mesh):
    in_specs = (
        P("client", None),
        P("client", None),
        P("client"),
        P("client"),
        P("cluster", None, None),
        P("cluster", None, None),
    )
    out_specs = (P("client", None), P("cluster", "client", None), P("cluster", "client", None))
    return jax.shard_map(body, mesh=mesh, in_specs=in_specs, out_specs=out_specs, check_vma=False)
```

profile of v0, /device:TPU:0, one launch (start us, length us, event | category | flops | bytes accessed | tf_op | source)
XLA Modules:
  0.0 122.5 jit_solution(4858923541895790107)
XLA Ops:
  7.2 0.0 copy-start
  7.2 0.0 reduce-scatter.2.cloned.1.call-start
  7.2 0.9 eq.21
  8.1 0.7 compare_select_fusion.1
  8.8 0.0 copy-start.1
  8.8 7.0 %convolution_convert_fusion = bf16[1536,512]{1,0:T(8,128)(2,1)S(1)} fusion(bf16[1536,2048]{1,0:T(8,128)(2,1)} %param.7, bf16[1,2048,512]{2,1,0:T(8,128)(2,1)} %param.11), kind=kOutput, calls=%fused_computation.7 | convolution fusion | flops 3222011904 | bytes 9961472 | tf_op jit(solution)/shard_map/dot_general | solution.py:31
  15.8 0.0 copy-done
  15.8 0.0 copy-done.1
  15.8 3.9 %multiply_convert_fusion = (bf16[1536,512]{1,0:T(8,128)(2,1)S(1)}, f32[1536,512]{1,0:T(8,128)S(1)}) fusion(bf16[1536,2048]{1,0:T(8,128)(2,1)S(1)} %copy-done.1, bf16[1,2048,512]{2,1,0:T(8,128)(2,1)S(1)} %copy-done), kind=kOutput, calls=%fused_computation.5 | convolution fusion | flops 3225157632 | bytes 13107200 | tf_op jit(solution)/shard_map/dot_general | solution.py:29
  19.7 0.6 fusion.9
  20.3 1.1 convolution_convert_fusion.1
  21.4 1.1 fusion.11
  22.5 0.0 slice-start
  22.5 1.1 fusion
  23.6 0.0 slice-start.1
  23.6 3.5 %convolution_bitcast_fusion.1 = f32[2048,512]{0,1:T(8,128)S(1)} fusion(bf16[1536,512]{1,0:T(8,128)(2,1)S(1)} %fusion, bf16[1536,2048]{1,0:T(8,128)(2,1)S(1)} %copy-done.1), kind=kOutput, calls=%fused_computation.2 | convolution fusion | flops 3221225472 | bytes 12058624 | tf_op jit(solution)/shard_map/dot_general | solution.py:15
  27.1 0.0 slice-done
  27.1 0.0 slice-done.1
  27.1 3.5 %convolution_bitcast_fusion = f32[2048,512]{0,1:T(8,128)S(1)} fusion(bf16[1536,512]{1,0:T(8,128)(2,1)S(1)} %bitcast.45, bf16[1536,2048]{1,0:T(8,128)(2,1)S(1)} %bitcast.44), kind=kOutput, calls=%fused_computation.1 | convolution fusion | flops 3221225472 | bytes 12058624 | tf_op jit(solution)/shard_map/dot_general | solution.py:15
  30.6 3.8 %pad_maximum_fusion = f32[2048,1024]{0,1:T(8,128)} fusion(f32[2048,512]{0,1:T(8,128)S(1)} %convolution_bitcast_fusion, f32[2048,512]{0,1:T(8,128)S(1)} %convolution_bitcast_fusion.1), kind=kLoop, calls=%fused_computation | loop fusion | flops 2097152 | bytes 16777216 | tf_op jit(solution)/shard_map/concatenate | solution.py:59
  34.4 0.0 reduce-scatter.2.cloned.1.call-update
  34.5 0.7 fusion.5
  35.2 22.3 %all-gather = f32[8,1,16]{2,1,0:T(1,128)S(1)} all-gather(f32[1,1,16]{2,1,0:T(1,128)S(1)} %multiply_bitcast_fusion), channel_id=1, replica_groups=mesh['cluster'=8,'client'=4] {'cluster'}, dimensions={0}, use_global_device_ids=true | all-gather | bytes 576 | tf_op jit(solution)/shard_map/all_gather | solution.py:44
  57.5 51.1 %reduce-scatter.2.cloned.1.call-done = f32[512,1024]{0,1:T(8,128)} async-done(((f32[2048,1024]{0,1:T(8,128)}), f32[512,1024]{0,1:T(8,128)}) %reduce-scatter.2.cloned.1.call-update) | async-done | bytes 2097168 | tf_op jit(solution)/shard_map/reduce_scatter | solution.py:58
  108.6 2.7 %slice_bitcast_fusion = (f32[1,512,512]{1,2,0:T(8,128)}, f32[1,512,512]{1,2,0:T(8,128)S(1)}) fusion(f32[512,1024]{0,1:T(8,128)} %reduce-scatter.2.cloned.1.call-done), kind=kLoop, calls=%fused_computation.13 | loop fusion | bytes 4194304 | tf_op jit(solution)/shard_map/broadcast_in_dim | solution.py:66
  111.3 2.5 %copy.14 = f32[1,512,512]{2,1,0:T(8,128)} copy(f32[1,512,512]{1,2,0:T(8,128)} %get-tuple-element.9) | data formatting | bytes 2097152
  113.8 1.3 %copy.13 = f32[1,512,512]{2,1,0:T(8,128)} copy(f32[1,512,512]{1,2,0:T(8,128)S(1)} %get-tuple-element.10) | data formatting | bytes 2097152
  115.1 0.6 copy.17
  (2 shorter events, 0.0 us)
Async XLA Ops:
  7.2 8.6 %copy-start = (bf16[1,2048,512]{2,1,0:T(8,128)(2,1)S(1)}, bf16[1,2048,512]{2,1,0:T(8,128)(2,1)}, u32[]{:S(2)}) copy-start(bf16[1,2048,512]{2,1,0:T(8,128)(2,1)} %param.10) | copy-start | bytes 6291460
  7.2 101.4 %reduce-scatter.2.cloned.1.call-start = ((), (), s32[]{:S(2)}) async-start(), calls=%async_computation.1 | async-start | bytes 10485760 | tf_op jit(solution)/shard_map/reduce_scatter | solution.py:58
  8.8 7.0 %copy-start.1 = (bf16[1536,2048]{1,0:T(8,128)(2,1)S(1)}, bf16[1536,2048]{1,0:T(8,128)(2,1)}, u32[]{:S(2)}) copy-start(bf16[1536,2048]{1,0:T(8,128)(2,1)} %param.6) | copy-start | bytes 18874372
  22.5 4.7 %slice-start = ((s8[6291456]{0:T(1024)(128)(4,1)}), s8[2097152]{0:T(1024)(128)(4,1)S(1)}, s32[]{:S(2)}) async-start(s8[6291456]{0:T(1024)(128)(4,1)} %bitcast.43), calls=%async_computation.2 | async-start | bytes 4194304
  23.6 3.5 %slice-start.1 = ((s8[6291456]{0:T(1024)(128)(4,1)}), s8[4194304]{0:T(1024)(128)(4,1)S(1)}, s32[]{:S(2)}) async-start(s8[6291456]{0:T(1024)(128)(4,1)} %bitcast.43), calls=%async_computation.3 | async-start | bytes 8388608
Sparse Core Ops, SparseCore 0:
  34.6 73.9 reduce-scatter.1
where the time goes:
time: 123 us
  waiting for transfers between devices  51.1 us (42%)
  blocking collectives  22.3 us (18%)
  matrix products  20.6 us (17%)
  between operations  14.1 us (11%)
  local copies, waits for them, and re-layouts  8.04 us (7%)
  other arithmetic  6.31 us (5%)
    reduce_scatter x1, waiting for transfers between devices, body(): lax.psum_scatter(jnp.concatenate([contract_rows(user_feats, pre_slope), c...  51.1 us
    all_gather x1, blocking collectives, body(): lax.all_gather(client_loss[:, None], 'cluster', axis=1, tiled=True)  22.3 us
    dot_general x1, matrix products, body(): jnp.dot(item_feats, item_map, preferred_element_type=jnp.float32)  6.99 us
    dot_general x2, matrix products, contract_rows(): lax.dot_general(left, right, (((0,), (0,)), ((), ())), preferred_element_...  6.96 us
    unnamed x11, local copies, waits for them, and re-layouts  4.46 us
    dot_general x1, matrix products, body(): pre_user = jnp.dot(user_feats, user_map, preferred_element_type=jnp.float32)  3.87 us
    concatenate x1, other arithmetic, body(): jnp.concatenate([contract_rows(user_feats, pre_slope), contract_rows(item...  3.8 us
    broadcast_in_dim x1, local copies, waits for them, and re-layouts, body(): partial_sum[None, :, width:]  2.68 us
  transfers between devices with their start and end apart: 1, of which 1 were waited for; matrix products, arithmetic and copies ran while one was open for 1% of the time, Pallas kernels for 0%

commit v1 on v0

v1 whole, which is shorter than its diff:
```python
import functools
import math

import jax
import jax.numpy as jnp
from jax import lax
from jax.experimental import pallas as pl
from jax.experimental.pallas import tpu as pltpu
from jax.sharding import PartitionSpec as P


GROUP = 4
EXACT = 8
LANES = 128


def contract_rows(left, right):
    return lax.dot_general(
        left, right, (((0,), (0,)), ((), ())), preferred_element_type=jnp.float32
    )


def contract_lanes(left, right):
    return lax.dot_general(
        left, right, (((1,), (1,)), ((), ())), preferred_element_type=jnp.float32
    )


def dot(left, right):
    return jnp.dot(left, right, preferred_element_type=jnp.float32)


def order_clients(picks_s, slots_s, clients, mine):
    chosen = jnp.int32(0)
    for c in range(clients):
        slots_s[chosen] = jnp.int32(c)
        chosen = chosen + (picks_s[c] == mine).astype(jnp.int32)
    last = chosen
    for c in range(clients):
        slots_s[last] = jnp.int32(c)
        last = last + (picks_s[c] != mine).astype(jnp.int32)
    return chosen


def label_block(ids_v, client, per):
    start = client * per
    row_at, off = start // LANES, start % LANES
    next_at = jnp.minimum(row_at + 1, ids_v.shape[0] - 1)
    lane = lax.broadcasted_iota(jnp.int32, (1, LANES), 1)
    turn = (LANES - off) % LANES
    here = pltpu.roll(ids_v[pl.ds(row_at, 1), :], turn, 1)
    there = pltpu.roll(ids_v[pl.ds(next_at, 1), :], turn, 1)
    row = jnp.where(lane < LANES - off, here, there).astype(jnp.float32)
    wide = jnp.broadcast_to(row, (per, LANES))
    diagonal = lax.broadcasted_iota(jnp.int32, (per, LANES), 0) == lax.broadcasted_iota(
        jnp.int32, (per, LANES), 1
    )
    column = jnp.sum(jnp.where(diagonal, wide, 0.0), axis=1, keepdims=True)
    return jnp.where(wide[:, :per] == column, 1.0, 0.0)


def run_user(at, feats, weight, user_v, bend_v):
    pre = dot(feats[at, :], weight[...])
    sig = jax.nn.sigmoid(pre)
    user_v[at, :] = (pre * sig).astype(jnp.bfloat16)
    if bend_v is not None:
        bend_v[at, :] = sig * (1.0 + pre * (1.0 - sig))


def run_item(at, feats, weight, item_v):
    item_v[at, :] = dot(feats[at, :], weight[...]).astype(jnp.bfloat16)


def scores_of(vectors, starts, per, temper):
    user_v, item_v = vectors
    users = [user_v[pl.ds(start, per), :] for start in starts]
    items = [item_v[pl.ds(start, per), :] for start in starts]
    scores = [contract_lanes(user, item) * temper for user, item in zip(users, items)]
    return users, items, scores


def run_slopes(base, slot, group, per, chosen, vectors, bend_v, label_v, slopes):
    user_slopes, item_slopes = slopes
    temper = 1.0 / math.sqrt(bend_v.shape[1])
    starts = [base + i * per for i in range(group)]
    users, items, scores = scores_of(vectors, starts, per, temper)
    slope = [
        ((jax.nn.sigmoid(score) - label_v[pl.ds(start, per), :per]) * jnp.where(slot + i < chosen, temper, 0.0)).astype(
            jnp.bfloat16
        )
        for i, (score, start) in enumerate(zip(scores, starts))
    ]
    for i, start in enumerate(starts):
        user_slopes[pl.ds(start, per), :] = (dot(slope[i], items[i]) * bend_v[pl.ds(start, per), :]).astype(jnp.bfloat16)
    for i, start in enumerate(starts):
        item_slopes[pl.ds(start, per), :] = contract_rows(slope[i], users[i]).astype(jnp.bfloat16)


def add_terms(feats, slopes, targets, span, cols, these, at, fresh):
    wide = cols.stop - cols.start
    for blocks, out in targets:
        for j, block in enumerate(blocks):
            place = (slice(j * span, (j + 1) * span), slice(at, at + wide))
            part_of = pl.ds(pl.multiple_of(block * span, span), span)
            part = contract_rows(feats[these, part_of], slopes[these, cols])
            out[place] = part if fresh else out[place] + part


def sum_terms(feats, slopes, targets, span, cols, groups, rows, at):
    @pl.when(groups == 1)
    def _():
        add_terms(feats, slopes, targets, span, cols, slice(0, rows), at, True)

    @pl.when(groups > 1)
    def _():
        add_terms(feats, slopes, targets, span, cols, slice(0, 2 * rows), at, True)

        def more(g, carry):
            add_terms(feats, slopes, targets, span, cols, pl.ds(pl.multiple_of(g * rows, rows), rows), at, False)
            return carry

        lax.fori_loop(2, groups, more, 0)


def relative_blocks(shards, flip):
    me = lax.axis_index("client")
    return [jnp.bitwise_xor(me, (j << 1) ^ flip) for j in range(shards // 4)]


def first_kernel(
    sizes, picks, ids_h, user_feats, item_feats, user_weight, item_weight,
    user_rows, item_rows, user_slopes, item_slopes, count_v, give, keep,
    picks_s, slots_s, ids_v, label_v, user_w, item_w, bend_v, user_v, item_v, small_sem, weight_sem, feat_sem,
):
    clients, per, group, shards, head = sizes
    rows = group * per
    mine = lax.axis_index("cluster")
    get_picks = pltpu.make_async_copy(picks, picks_s, small_sem.at[0])
    get_ids = pltpu.make_async_copy(ids_h, ids_v, small_sem.at[1])
    get_user_w = pltpu.make_async_copy(user_weight.at[0], user_w, weight_sem.at[0])
    get_item_w = pltpu.make_async_copy(item_weight.at[0], item_w, weight_sem.at[1])
    get_picks.start()
    get_user_w.start()
    get_picks.wait()
    chosen = order_clients(picks_s, slots_s, clients, mine)
    live = jnp.maximum(1, chosen)
    groups = (live + group - 1) // group
    feats, slopes = (user_rows, item_rows), (user_slopes, item_slopes)

    def place_of(slot):
        return pl.ds(pl.multiple_of(slot * per, per), per)

    def get_rows(tower, slot):
        source = (user_feats, item_feats)[tower]
        return pltpu.make_async_copy(
            source.at[place_of(slots_s[slot]), :], feats[tower].at[place_of(slot), :], feat_sem.at[tower, slot]
        )

    def start_rows(tower):
        def start(slot, carry):
            get_rows(tower, slot).start()
            return carry

        lax.fori_loop(0, live, start, 0)

    start_rows(0)
    get_item_w.start()
    start_rows(1)
    get_ids.start()
    count_v[...] = jnp.broadcast_to(groups.astype(jnp.float32), count_v.shape)

    def clear(slot, carry):
        for tower in range(2):
            feats[tower][place_of(slot), :] = jnp.zeros((per, user_rows.shape[1]), jnp.bfloat16)
            slopes[tower][place_of(slot), :] = jnp.zeros((per, user_slopes.shape[1]), jnp.bfloat16)
        return carry

    lax.fori_loop(live, groups * group, clear, 0)
    get_ids.wait()

    def label_group(g, carry):
        for i in range(group):
            slot = g * group + i
            label_v[place_of(slot), :per] = label_block(ids_v, slots_s[slot], per)
        return carry

    lax.fori_loop(0, groups, label_group, 0)

    top = shards // 2
    span = user_rows.shape[1] // shards
    targets = ((relative_blocks(shards, top ^ 1), give), (relative_blocks(shards, top), keep))

    def slopes_of(base, slot, number):
        run_slopes(base, slot, number, per, chosen, (user_v, item_v), bend_v, label_v, slopes)

    def run_exactly(number):
        these = slice(0, number * per)
        get_user_w.wait()
        for slot in range(number):
            get_rows(0, slot).wait()
        run_user(these, user_rows, user_w, user_v, bend_v)
        get_item_w.wait()
        for slot in range(number):
            get_rows(1, slot).wait()
        run_item(these, item_rows, item_w, item_v)
        slopes_of(0, 0, number)
        add_terms(user_rows, user_slopes, targets, span, slice(0, head), these, 0, True)

    def run_groups():
        def of_group(work):
            def run(g, carry):
                work(g, pl.ds(pl.multiple_of(g * rows, rows), rows))
                return carry

            return lambda: lax.fori_loop(0, groups, run, 0)

        def await_rows(tower):
            def wait(slot, carry):
                get_rows(tower, slot).wait()
                return carry

            lax.fori_loop(0, live, wait, 0)

        get_user_w.wait()
        await_rows(0)
        of_group(lambda g, these: run_user(these, user_rows, user_w, user_v, bend_v))()
        get_item_w.wait()
        await_rows(1)
        of_group(lambda g, these: run_item(these, item_rows, item_w, item_v))()
        of_group(lambda g, these: slopes_of(pl.multiple_of(g * rows, rows), g * group, group))()
        sum_terms(user_rows, user_slopes, targets, span, slice(0, head), groups, rows, 0)

    exact = min(EXACT, clients)
    for number in range(1, exact + 1):
        pl.when(live == number)(functools.partial(run_exactly, number))
    if exact < clients:
        pl.when(live > exact)(run_groups)


def terms_kernel(sizes, user_rows, item_rows, user_slopes, item_slopes, count_v, after, give, *keeps):
    rows, shards, flip, skip = sizes
    del after
    groups = jnp.max(count_v[...]).astype(jnp.int32)
    span = user_rows.shape[1] // shards
    width = user_slopes.shape[1]
    towers = ((user_rows, user_slopes, slice(skip, width)), (item_rows, item_slopes, slice(0, width)))
    at = 0
    for tower, (feats, slopes, cols) in enumerate(towers):
        sum_terms(feats, slopes, ((relative_blocks(shards, flip ^ 1), give),), span, cols, groups, rows, at)
        sum_terms(feats, slopes, ((relative_blocks(shards, flip), keeps[tower]),), span, cols, groups, rows, 0)
        at += cols.stop - cols.start


def loss_kernel(sizes, ids_v, user_feats, item_feats, user_weight, item_weight, after, loss_v, user_v, item_v):
    per, group = sizes
    del after
    g = pl.program_id(0)
    mine = lax.axis_index("cluster")
    temper = 1.0 / math.sqrt(user_v.shape[1])
    everything = slice(0, group * per)
    run_user(everything, user_feats, user_weight.at[0], user_v, None)
    run_item(everything, item_feats, item_weight.at[0], item_v)
    lane = lax.broadcasted_iota(jnp.int32, loss_v.shape, 1)
    row = lax.broadcasted_iota(jnp.int32, loss_v.shape, 0)
    _, _, scores = scores_of((user_v, item_v), [i * per for i in range(group)], per, temper)
    losses = jnp.where(g == 0, 0.0, loss_v[...])
    for i, score in enumerate(scores):
        client = g * group + i
        labels = label_block(ids_v, client, per)
        soft = jnp.maximum(score, 0.0) + jnp.log1p(jnp.exp(-jnp.abs(score)))
        pair = soft - labels * score
        loss = jnp.sum(jnp.sum(pair, axis=1, keepdims=True), axis=0, keepdims=True) / (per * per)
        losses = jnp.where((row == mine) & (lane == client), loss, losses)
    loss_v[...] = losses


def swapped(value, axis, mask, size):
    return lax.ppermute(value, axis, [(i, i ^ mask) for i in range(size)])


def in_vmem(value):
    return pltpu.with_memory_space_constraint(value, pltpu.VMEM)


def in_hbm(*values):
    return [pltpu.with_memory_space_constraint(value, pltpu.HBM) for value in values]


def body(sizes, user_feats, item_feats, item_ids, picks, user_weight, item_weight):
    shards, clusters = sizes
    clients = picks.shape[0]
    row_count, depth = user_feats.shape
    per = row_count // clients
    width = user_weight.shape[2]
    group = math.gcd(clients, GROUP)
    rows = group * per
    head = width // 2
    top = shards // 2
    quarter = depth // 4
    table_rows = -(-clusters // 8) * 8
    assert shards & (shards - 1) == 0 and shards >= 4 and per <= LANES and clients <= LANES

    ids = item_ids.reshape(-1, LANES)
    bf16, f32, i32 = jnp.bfloat16, jnp.float32, jnp.int32
    hbm = pl.BlockSpec(memory_space=pltpu.HBM)
    anywhere = pl.BlockSpec(memory_space=pl.ANY)
    vmem = pl.BlockSpec(memory_space=pltpu.VMEM)
    flops = 2 * rows * depth * width

    def cost(factor):
        return pl.CostEstimate(flops=int(factor * flops), bytes_accessed=1 << 20, transcendentals=0)

    def params(mib):
        return pltpu.CompilerParams(vmem_limit_bytes=mib << 20)

    user_rows, item_rows, user_slopes, item_slopes, count, give, keep = pl.pallas_call(
        functools.partial(first_kernel, (clients, per, group, shards, head)),
        out_shape=[
            pltpu.VMEM((row_count, depth), bf16),
            pltpu.VMEM((row_count, depth), bf16),
            pltpu.VMEM((row_count, width), bf16),
            pltpu.VMEM((row_count, width), bf16),
            pltpu.VMEM((8, LANES), f32),
            pltpu.VMEM((quarter, head), f32),
            pltpu.VMEM((quarter, head), f32),
        ],
        in_specs=[hbm] * 6,
        out_specs=[vmem] * 7,
        scratch_shapes=[
            pltpu.SMEM((clients,), i32),
            pltpu.SMEM((clients + 1,), i32),
            pltpu.VMEM(ids.shape, i32),
            pltpu.VMEM((row_count, LANES), f32),
            pltpu.VMEM((depth, width), bf16),
            pltpu.VMEM((depth, width), bf16),
            pltpu.VMEM((row_count, width), f32),
            pltpu.VMEM((row_count, width), bf16),
            pltpu.VMEM((row_count, width), bf16),
            pltpu.SemaphoreType.DMA((2,)),
            pltpu.SemaphoreType.DMA((2,)),
            pltpu.SemaphoreType.DMA((2, clients)),
        ],
        compiler_params=params(24),
        cost_estimate=cost(6),
        name="first",
    )(*in_hbm(picks, ids, user_feats, item_feats, user_weight, item_weight))

    def terms(flip, skip, after):
        return pl.pallas_call(
            functools.partial(terms_kernel, (rows, shards, flip, skip)),
            out_shape=[
                pltpu.VMEM((quarter, 2 * width - skip), f32),
                pltpu.VMEM((quarter, width - skip), f32),
                pltpu.VMEM((quarter, width), f32),
            ],
            in_specs=[vmem] * 5 + [anywhere],
            out_specs=[vmem] * 3,
            compiler_params=params(8),
            cost_estimate=cost(2),
        )(in_vmem(user_rows), in_vmem(item_rows), in_vmem(user_slopes), in_vmem(item_slopes), in_vmem(count), after)

    def swap(value, axis, mask):
        return swapped(value, axis, mask, shards if axis == "client" else clusters)

    first_sum = swap(give, "client", 1) + keep
    from_first = swap(first_sum, "client", top)

    give, keep_user, keep_item = terms(top, head, count)
    got = swap(give, "client", 1)
    second_sum = got[:, : width - head] + keep_user
    third_sum = got[:, width - head :] + keep_item
    from_second = swap(second_sum, "client", top)
    from_third = swap(third_sum, "client", top)

    give, keep_user, keep_item = terms(0, 0, first_sum)
    got = swap(give, "client", 1)

    whole = lambda *shape: pl.BlockSpec(shape, lambda g: (0,) * len(shape))
    loss = pl.pallas_call(
        functools.partial(loss_kernel, (per, group)),
        grid=(clients // group,),
        out_shape=jax.ShapeDtypeStruct((table_rows, LANES), f32),
        in_specs=[
            whole(*ids.shape),
            pl.BlockSpec((rows, depth), lambda g: (g, 0)),
            pl.BlockSpec((rows, depth), lambda g: (g, 0)),
            whole(1, depth, width),
            whole(1, depth, width),
            anywhere,
        ],
        out_specs=whole(table_rows, LANES),
        scratch_shapes=[pltpu.VMEM((rows, width), bf16), pltpu.VMEM((rows, width), bf16)],
        compiler_params=params(24),
        cost_estimate=cost(8),
        name="loss",
    )(*in_hbm(ids, user_feats, item_feats, user_weight, item_weight), third_sum)
    home_user = got[:, :width] + keep_user
    home_item = got[:, width:] + keep_item
    loss, home_user, home_item = lax.optimization_barrier((loss, home_user, home_item))
    mask = 1
    while mask < clusters:
        loss = loss + swap(loss, "cluster", mask)
        mask *= 2
    loss_table = loss[:clusters, :clients].T

    user_grad = home_user + jnp.concatenate([from_first, from_second], axis=1)
    from_third, user_grad = lax.optimization_barrier((from_third, user_grad))
    item_grad = home_item + from_third
    half = shards // 4
    while half > 1:
        half //= 2
        cut = half * (depth // shards)
        mask = half << 1
        user_grad = user_grad[:cut] + swapped(user_grad[cut:], "client", mask, shards)
        item_grad = item_grad[:cut] + swapped(item_grad[cut:], "client", mask, shards)
    return loss_table, user_grad[None], item_grad[None]


def solution(mesh):
    in_specs = (
        P("client", None),
        P("client", None),
        P("client"),
        P("client"),
        P("cluster", None, None),
        P("cluster", None, None),
    )
    out_specs = (P("client", None), P("cluster", "client", None), P("cluster", "client", None))
    sizes = (mesh.shape["client"], mesh.shape["cluster"])
    return jax.shard_map(
        functools.partial(body, sizes), mesh=mesh, in_specs=in_specs, out_specs=out_specs, check_vma=False
    )
```

time: 123 us -> 69 us (0.56)
  the two profiles are of different devices: /device:TPU:0 before, /device:TPU:30 now
where the time goes in v1:
time: 69 us; the launch traced here: 68.8 us
  waiting for transfers between devices  35.5 us (51%)
  Pallas kernels  25.8 us (37%)
  other arithmetic  3.1 us (4%)
  starting transfers between devices  3.01 us (4%)
  between operations  0.72 us (1%)
    ppermute x9, waiting for transfers between devices, swapped(): return lax.ppermute(value, axis, [(i, i ^ mask) for i in range(size)])  35.5 us
    pallas_call x1, Pallas kernels, body(): pl.pallas_call(functools.partial(loss_kernel, (per, group)), grid=(client...  11.6 us
    pallas_call x1, Pallas kernels, body(): pl.pallas_call(functools.partial(first_kernel, (clients, per, group, shar...  9.16 us
    pallas_call x2, Pallas kernels, terms(): pl.pallas_call(functools.partial(terms_kernel, (rows, shards, flip, skip)...  5.02 us
    ppermute x9, starting transfers between devices, swapped(): return lax.ppermute(value, axis, [(i, i ^ mask) for i in range(size)])  3.01 us
  transfers between devices with their start and end apart: 9, of which 5 were waited for; matrix products, arithmetic and copies ran while one was open for 5% of the time, Pallas kernels for 24%

profile of v1, /device:TPU:30, one launch (start us, length us, event | category | flops | bytes accessed | tf_op | source)
XLA Modules:
  0.0 68.8 jit_solution(11871304881934116153)
XLA Ops:
  0.6 9.2 %first.1 = (bf16[1536,2048]{1,0:T(8,128)(2,1)S(1)}, bf16[1536,2048]{1,0:T(8,128)(2,1)S(1)}, bf16[1536,512]{1,0:T(8,128)(2,1)S(1)}, bf16[1536,512]{1,0:T(8,128)(2...) custom-call(s32[16]{0:T(128)} %picks.1, s32[12,128]{1,0:T(8,128)} %bitcast.7, ...), custom_call_target="tpu_custom_call" | custom-call | flops 4831838208 | bytes 1048576 | tf_op jit(solution)/shard_map/first/pallas_call | solution.py:316
  9.8 0.1 collective-permute-start.1
  9.9 2.4 %shard_map.85 = (f32[512,768]{1,0:T(8,128)S(1)}, f32[512,256]{1,0:T(8,128)S(1)}, f32[512,512]{1,0:T(8,128)S(1)}) custom-call(bf16[1536,2048]{1,0:T(8,128)(2,1)S(1)} %get-tuple-element.21.user_rows, bf16[1536,2048]{1,0:T(8,128)(2,1)S(1)} %get-tuple-element.22.item_rows, bf16[1536,512]{1,0:T(8,128)(2,1)S(1)} %get-tuple-element.23.user_slopes, ...), custom_call_target="tpu_custom_call" | custom-call | flops 1610612736 | bytes 1048576 | tf_op jit(solution)/shard_map/pallas_call | solution.py:349
  12.3 0.6 collective-permute-start
  12.9 0.0 collective-permute-done.1
  12.9 0.1 add.31.after
  13.0 2.6 %shard_map.86 = (f32[512,1024]{1,0:T(8,128)S(1)}, f32[512,512]{1,0:T(8,128)S(1)}, f32[512,512]{1,0:T(8,128)S(1)}) custom-call(bf16[1536,2048]{1,0:T(8,128)(2,1)S(1)} %get-tuple-element.21.user_rows, bf16[1536,2048]{1,0:T(8,128)(2,1)S(1)} %get-tuple-element.22.item_rows, bf16[1536,512]{1,0:T(8,128)(2,1)S(1)} %get-tuple-element.23.user_slopes, ...), custom_call_target="tpu_custom_call" | custom-call | flops 1610612736 | bytes 1048576 | tf_op jit(solution)/shard_map/pallas_call | solution.py:349
  15.5 0.1 collective-permute-start.2
  15.6 0.1 collective-permute-start.7
  15.7 0.2 collective-permute-done
  15.9 0.1 slice_add_fusion.3
  16.0 1.9 %collective-permute-start.8 = (f32[512,256]{1,0:T(8,128)S(1)}, f32[512,256]{1,0:T(8,128)S(1)}, u32[]{:S(2)}, u32[]{:S(2)}) collective-permute-start(f32[512,256]{1,0:T(8,128)S(1)} %slice_add_fusion.3), channel_id=1, source_target_pairs={{0,2},{1,3},{2,0},{3,1},{4,6},{5,7},{6,4},{7,5},{8,10},{9,11},{10,... | collective-permute-start | bytes 1572872 | tf_op jit(solution)/shard_map/ppermute | solution.py:278
  17.9 0.2 slice_add_fusion.2.after
  18.0 0.3 collective-permute-start.6
  18.3 11.6 %loss.1 = f32[8,128]{1,0:T(8,128)S(1)} custom-call(s32[12,128]{1,0:T(8,128)} %bitcast.8, bf16[1536,2048]{1,0:T(8,128)(2,1)} %user_feats.3, bf16[1536,2048]{1,0:T(8,128)(2,1)} %item_feats.3, bf16[1,2048,512]{2,1,0:T(8,128)(2,1)} %user_weight.3, bf16[1,2048,512]{2,1,0:T(8,128)(2,1)} %item_weight.3, f32[512,512]{1,0:T(8,128)S(1)} %slice_add_fusion.2.after), custom_call_target="tpu_custom_call" | custom-call | flops 6442450944 | bytes 1048576 | tf_op jit(solution)/shard_map/loss/pallas_call | solution.py:379
  29.9 0.0 collective-permute-done.2
  30.0 0.5 slice_add_fusion
  30.4 0.1 collective-permute-start.3
  30.5 3.6 %collective-permute-done.3 = f32[8,128]{1,0:T(8,128)S(1)} collective-permute-done((f32[8,128]{1,0:T(8,128)S(1)}, f32[8,128]{1,0:T(8,128)S(1)}, u32[]{:S(2)}, u32[]{:S(2)}) %collective-permute-start.3) | collective-permute-done | bytes 4128 | tf_op jit(solution)/shard_map/ppermute | solution.py:278
  34.1 0.0 collective-permute-start.4
  34.1 0.0 collective-permute-done.7
  34.1 7.6 %collective-permute-done.8 = f32[512,256]{1,0:T(8,128)S(1)} collective-permute-done((f32[512,256]{1,0:T(8,128)S(1)}, f32[512,256]{1,0:T(8,128)S(1)}, u32[]{:S(2)}, u32[]{:S(2)}) %collective-permute-start.8) | collective-permute-done | bytes 524320 | tf_op jit(solution)/shard_map/ppermute | solution.py:278
  41.7 1.1 %maximum_add_fusion = f32[512,512]{1,0:T(8,128)} fusion(f32[512,512]{1,0:T(8,128)S(1)} %get-tuple-element.34, f32[512,256]{1,0:T(8,128)S(1)} %collective-permute-done.8, f32[512,256]{1,0:T(8,128)S(1)} %collective-permute-done.7), kind=kLoop, calls=%fused_computation.3 | loop fusion | flops 524288 | bytes 3145728 | tf_op jit(solution)/shard_map/add | solution.py:406
  42.9 20.8 %collective-permute-done.6 = f32[512,512]{1,0:T(8,128)S(1)} collective-permute-done((f32[512,512]{1,0:T(8,128)S(1)}, f32[512,512]{1,0:T(8,128)S(1)}, u32[]{:S(2)}, u32[]{:S(2)}) %collective-permute-start.6) | collective-permute-done | bytes 1048608 | tf_op jit(solution)/shard_map/ppermute | solution.py:278
  63.7 0.0 collective-permute-done.4
  63.7 0.0 collective-permute-start.5
  63.7 1.2 %add_bitcast_fusion = f32[1,512,512]{2,1,0:T(8,128)} fusion(f32[512,512]{1,0:T(8,128)S(1)} %get-tuple-element.37, f32[512,512]{1,0:T(8,128)S(1)} %collective-permute-done.6), kind=kLoop, calls=%fused_computation.4 | loop fusion | flops 262144 | bytes 3145728 | tf_op jit(solution)/shard_map/broadcast_in_dim | solution.py:416
  64.8 3.3 %collective-permute-done.5 = f32[8,128]{1,0:T(8,128)S(1)} collective-permute-done((f32[8,128]{1,0:T(8,128)S(1)}, f32[8,128]{1,0:T(8,128)S(1)}, u32[]{:S(2)}, u32[]{:S(2)}) %collective-permute-start.5) | collective-permute-done | bytes 4128 | tf_op jit(solution)/shard_map/ppermute | solution.py:278
  68.2 0.6 slice_bitcast_fusion
  (3 shorter events, 0.0 us)
Async XLA Ops:
  9.8 3.1 %collective-permute-start.1 = (f32[512,256]{1,0:T(8,128)S(1)}, f32[512,256]{1,0:T(8,128)S(1)}, u32[]{:S(2)}, u32[]{:S(2)}) collective-permute-start(f32[512,256]{1,0:T(8,128)S(1)} %get-tuple-element.28), channel_id=1, source_target_pairs={{0,1},{1,0},{2,3},{3,2},{4,5},{5,4},{6,7},{7,6},{8,9},{9,8},{10,11... | collective-permute-start | bytes 1572872 | tf_op jit(solution)/shard_map/ppermute | solution.py:278
  12.3 3.6 %collective-permute-start = (f32[512,768]{1,0:T(8,128)S(1)}, f32[512,768]{1,0:T(8,128)S(1)}, u32[]{:S(2)}, u32[]{:S(2)}) collective-permute-start(f32[512,768]{1,0:T(8,128)S(1)} %get-tuple-element.26), channel_id=1, source_target_pairs={{0,1},{1,0},{2,3},{3,2},{4,5},{5,4},{6,7},{7,6},{8,9},{9,8},{10,11... | collective-permute-start | bytes 4718600 | tf_op jit(solution)/shard_map/ppermute | solution.py:278
  15.5 14.4 %collective-permute-start.2 = (f32[512,1024]{1,0:T(8,128)S(1)}, f32[512,1024]{1,0:T(8,128)S(1)}, u32[]{:S(2)}, u32[]{:S(2)}) collective-permute-start(f32[512,1024]{1,0:T(8,128)S(1)} %get-tuple-element.30), channel_id=1, source_target_pairs={{0,1},{1,0},{2,3},{3,2},{4,5},{5,4},{6,7},{7,6},{8,9},{9,8},{10,11... | collective-permute-start | bytes 6291464 | tf_op jit(solution)/shard_map/ppermute | solution.py:278
  15.6 18.5 %collective-permute-start.7 = (f32[512,256]{1,0:T(8,128)S(1)}, f32[512,256]{1,0:T(8,128)S(1)}, u32[]{:S(2)}, u32[]{:S(2)}) collective-permute-start(f32[512,256]{1,0:T(8,128)S(1)} %add.31.after), channel_id=1, source_target_pairs={{0,2},{1,3},{2,0},{3,1},{4,6},{5,7},{6,4},{7,5},{8,10},{9,11},{10,... | collective-permute-start | bytes 1572872 | tf_op jit(solution)/shard_map/ppermute | solution.py:278
  16.0 25.7 %collective-permute-start.8 = (f32[512,256]{1,0:T(8,128)S(1)}, f32[512,256]{1,0:T(8,128)S(1)}, u32[]{:S(2)}, u32[]{:S(2)}) collective-permute-start(f32[512,256]{1,0:T(8,128)S(1)} %slice_add_fusion.3), channel_id=1, source_target_pairs={{0,2},{1,3},{2,0},{3,1},{4,6},{5,7},{6,4},{7,5},{8,10},{9,11},{10,... | collective-permute-start | bytes 1572872 | tf_op jit(solution)/shard_map/ppermute | solution.py:278
  18.0 45.6 %collective-permute-start.6 = (f32[512,512]{1,0:T(8,128)S(1)}, f32[512,512]{1,0:T(8,128)S(1)}, u32[]{:S(2)}, u32[]{:S(2)}) collective-permute-start(f32[512,512]{1,0:T(8,128)S(1)} %slice_add_fusion.2.after), channel_id=1, source_target_pairs={{0,2},{1,3},{2,0},{3,1},{4,6},{5,7},{6,4},{7,5},{8,10},{9,11},{10,... | collective-permute-start | bytes 3145736 | tf_op jit(solution)/shard_map/ppermute | solution.py:278
  30.4 3.7 %collective-permute-start.3 = (f32[8,128]{1,0:T(8,128)S(1)}, f32[8,128]{1,0:T(8,128)S(1)}, u32[]{:S(2)}, u32[]{:S(2)}) collective-permute-start(f32[8,128]{1,0:T(8,128)S(1)} %loss.1), channel_id=1, source_target_pairs={{0,4},{4,0},{8,12},{12,8},{16,20},{20,16},{24,28},{28,24},{1,5},{5... | collective-permute-start | bytes 12296 | tf_op jit(solution)/shard_map/ppermute | solution.py:278
  34.1 29.5 %collective-permute-start.4 = (f32[8,128]{1,0:T(8,128)S(1)}, f32[8,128]{1,0:T(8,128)S(1)}, u32[]{:S(2)}, u32[]{:S(2)}) collective-permute-start(f32[8,128]{1,0:T(8,128)S(1)} %add.34), channel_id=1, source_target_pairs={{0,8},{4,12},{8,0},{12,4},{16,24},{20,28},{24,16},{28,20},{1,9},{5... | collective-permute-start | bytes 12296 | tf_op jit(solution)/shard_map/ppermute | solution.py:278
  63.7 4.5 %collective-permute-start.5 = (f32[8,128]{1,0:T(8,128)S(1)}, f32[8,128]{1,0:T(8,128)S(1)}, u32[]{:S(2)}, u32[]{:S(2)}) collective-permute-start(f32[8,128]{1,0:T(8,128)S(1)} %add.35), channel_id=1, source_target_pairs={{0,16},{4,20},{8,24},{12,28},{16,0},{20,4},{24,8},{28,12},{1,17},{... | collective-permute-start | bytes 12296 | tf_op jit(solution)/shard_map/ppermute | solution.py:278

commit v2 on v1

--- a/solution.py
+++ b/solution.py
@@ -11,6 +11,7 @@
 
 GROUP = 4
 EXACT = 8
+HEAD = 4
 LANES = 128
 
 
@@ -79,21 +80,25 @@
     return users, items, scores
 
 
-def run_slopes(base, slot, group, per, chosen, vectors, bend_v, label_v, slopes):
-    user_slopes, item_slopes = slopes
-    temper = 1.0 / math.sqrt(bend_v.shape[1])
+def run_item_slopes(base, slot, group, per, chosen, vectors, label_v, slope_v, item_slopes):
+    temper = 1.0 / math.sqrt(item_slopes.shape[1])
     starts = [base + i * per for i in range(group)]
-    users, items, scores = scores_of(vectors, starts, per, temper)
-    slope = [
+    users, _, scores = scores_of(vectors, starts, per, temper)
+    slopes = [
         ((jax.nn.sigmoid(score) - label_v[pl.ds(start, per), :per]) * jnp.where(slot + i < chosen, temper, 0.0)).astype(
             jnp.bfloat16
         )
         for i, (score, start) in enumerate(zip(scores, starts))
     ]
-    for i, start in enumerate(starts):
-        user_slopes[pl.ds(start, per), :] = (dot(slope[i], items[i]) * bend_v[pl.ds(start, per), :]).astype(jnp.bfloat16)
-    for i, start in enumerate(starts):
-        item_slopes[pl.ds(start, per), :] = contract_rows(slope[i], users[i]).astype(jnp.bfloat16)
+    for slope, user, start in zip(slopes, users, starts):
+        item_slopes[pl.ds(start, per), :] = contract_rows(slope, user).astype(jnp.bfloat16)
+        slope_v[pl.ds(start, per), :per] = slope
+
+
+def run_user_slopes(base, group, per, slope_v, item_v, bend_v, user_slopes):
+    for i in range(group):
+        at = pl.ds(base + i * per, per)
+        user_slopes[at, :] = (dot(slope_v[at, :per], item_v[at, :]) * bend_v[at, :]).astype(jnp.bfloat16)
 
 
 def add_terms(feats, slopes, targets, span, cols, these, at, fresh):
@@ -129,8 +134,8 @@
 
 def first_kernel(
     sizes, picks, ids_h, user_feats, item_feats, user_weight, item_weight,
-    user_rows, item_rows, user_slopes, item_slopes, count_v, give, keep,
-    picks_s, slots_s, ids_v, label_v, user_w, item_w, bend_v, user_v, item_v, small_sem, weight_sem, feat_sem,
+    user_rows, item_rows, slope_v, bend_v, item_v, item_slopes, count_v, give, keep,
+    picks_s, slots_s, ids_v, label_v, user_w, item_w, user_v, small_sem, weight_sem, feat_sem,
 ):
     clients, per, group, shards, head = sizes
     rows = group * per
@@ -141,11 +146,12 @@
     get_item_w = pltpu.make_async_copy(item_weight.at[0], item_w, weight_sem.at[1])
     get_picks.start()
     get_user_w.start()
+    get_ids.start()
     get_picks.wait()
     chosen = order_clients(picks_s, slots_s, clients, mine)
     live = jnp.maximum(1, chosen)
     groups = (live + group - 1) // group
-    feats, slopes = (user_rows, item_rows), (user_slopes, item_slopes)
+    feats = (user_rows, item_rows)
 
     def place_of(slot):
         return pl.ds(pl.multiple_of(slot * per, per), per)
@@ -164,15 +170,11 @@
         lax.fori_loop(0, live, start, 0)
 
     start_rows(0)
-    get_item_w.start()
-    start_rows(1)
-    get_ids.start()
     count_v[...] = jnp.broadcast_to(groups.astype(jnp.float32), count_v.shape)
 
     def clear(slot, carry):
-        for tower in range(2):
-            feats[tower][place_of(slot), :] = jnp.zeros((per, user_rows.shape[1]), jnp.bfloat16)
-            slopes[tower][place_of(slot), :] = jnp.zeros((per, user_slopes.shape[1]), jnp.bfloat16)
+        for ref in (user_rows, item_rows, slope_v, bend_v, item_v, item_slopes):
+            ref[place_of(slot), :] = jnp.zeros((per, ref.shape[1]), ref.dtype)
         return carry
 
     lax.fori_loop(live, groups * group, clear, 0)
@@ -185,26 +187,28 @@
         return carry
 
     lax.fori_loop(0, groups, label_group, 0)
+    get_user_w.wait()
+    get_item_w.start()
 
     top = shards // 2
     span = user_rows.shape[1] // shards
     targets = ((relative_blocks(shards, top ^ 1), give), (relative_blocks(shards, top), keep))
 
     def slopes_of(base, slot, number):
-        run_slopes(base, slot, number, per, chosen, (user_v, item_v), bend_v, label_v, slopes)
+        run_item_slopes(base, slot, number, per, chosen, (user_v, item_v), label_v, slope_v, item_slopes)
 
     def run_exactly(number):
         these = slice(0, number * per)
-        get_user_w.wait()
         for slot in range(number):
             get_rows(0, slot).wait()
+        start_rows(1)
         run_user(these, user_rows, user_w, user_v, bend_v)
         get_item_w.wait()
         for slot in range(number):
             get_rows(1, slot).wait()
         run_item(these, item_rows, item_w, item_v)
         slopes_of(0, 0, number)
-        add_terms(user_rows, user_slopes, targets, span, slice(0, head), these, 0, True)
+        add_terms(item_rows, item_slopes, targets, span, slice(0, head), these, 0, True)
 
     def run_groups():
         def of_group(work):
@@ -221,14 +225,14 @@
 
             lax.fori_loop(0, live, wait, 0)
 
-        get_user_w.wait()
         await_rows(0)
+        start_rows(1)
         of_group(lambda g, these: run_user(these, user_rows, user_w, user_v, bend_v))()
         get_item_w.wait()
         await_rows(1)
         of_group(lambda g, these: run_item(these, item_rows, item_w, item_v))()
         of_group(lambda g, these: slopes_of(pl.multiple_of(g * rows, rows), g * group, group))()
-        sum_terms(user_rows, user_slopes, targets, span, slice(0, head), groups, rows, 0)
+        sum_terms(item_rows, item_slopes, targets, span, slice(0, head), groups, rows, 0)
 
     exact = min(EXACT, clients)
     for number in range(1, exact + 1):
@@ -237,18 +241,47 @@
         pl.when(live > exact)(run_groups)
 
 
-def terms_kernel(sizes, user_rows, item_rows, user_slopes, item_slopes, count_v, after, give, *keeps):
-    rows, shards, flip, skip = sizes
+def both_targets(shards, flip, give, keep):
+    return ((relative_blocks(shards, flip ^ 1), give), (relative_blocks(shards, flip), keep))
+
+
+def groups_of(count_v):
+    return jnp.max(count_v[...]).astype(jnp.int32)
+
+
+def item_kernel(sizes, item_rows, item_slopes, count_v, after, give, keep):
+    rows, shards, head = sizes
     del after
-    groups = jnp.max(count_v[...]).astype(jnp.int32)
-    span = user_rows.shape[1] // shards
+    cols = slice(head, item_slopes.shape[1])
+    targets = both_targets(shards, shards // 2, give, keep)
+    sum_terms(item_rows, item_slopes, targets, item_rows.shape[1] // shards, cols, groups_of(count_v), rows, 0)
+
+
+def user_kernel(sizes, user_rows, slope_v, bend_v, item_v, count_v, user_slopes, give, keep):
+    per, rows, shards = sizes
+    groups = groups_of(count_v)
+
+    def slopes(g, carry):
+        run_user_slopes(pl.multiple_of(g * rows, rows), rows // per, per, slope_v, item_v, bend_v, user_slopes)
+        return carry
+
+    lax.fori_loop(0, groups, slopes, 0)
+    targets = both_targets(shards, shards // 2, give, keep)
+    cols = slice(0, user_slopes.shape[1])
+    sum_terms(user_rows, user_slopes, targets, user_rows.shape[1] // shards, cols, groups, rows, 0)
+
+
+def home_kernel(sizes, user_rows, item_rows, user_slopes, item_slopes, count_v, after, give, keep_user, keep_item):
+    rows, shards = sizes
+    del after
+    groups = groups_of(count_v)
     width = user_slopes.shape[1]
-    towers = ((user_rows, user_slopes, slice(skip, width)), (item_rows, item_slopes, slice(0, width)))
-    at = 0
-    for tower, (feats, slopes, cols) in enumerate(towers):
-        sum_terms(feats, slopes, ((relative_blocks(shards, flip ^ 1), give),), span, cols, groups, rows, at)
-        sum_terms(feats, slopes, ((relative_blocks(shards, flip), keeps[tower]),), span, cols, groups, rows, 0)
-        at += cols.stop - cols.start
+    towers = ((user_rows, user_slopes, keep_user), (item_rows, item_slopes, keep_item))
+    for tower, (feats, slopes, keep) in enumerate(towers):
+        span = feats.shape[1] // shards
+        cols = slice(0, width)
+        sum_terms(feats, slopes, ((relative_blocks(shards, 1), give),), span, cols, groups, rows, tower * width)
+        sum_terms(feats, slopes, ((relative_blocks(shards, 0), keep),), span, cols, groups, rows, 0)
 
 
 def loss_kernel(sizes, ids_v, user_feats, item_feats, user_weight, item_weight, after, loss_v, user_v, item_v):
@@ -294,7 +327,7 @@
     width = user_weight.shape[2]
     group = math.gcd(clients, GROUP)
     rows = group * per
-    head = width // 2
+    head = width // HEAD
     top = shards // 2
     quarter = depth // 4
     table_rows = -(-clusters // 8) * 8
@@ -313,19 +346,33 @@
     def params(mib):
         return pltpu.CompilerParams(vmem_limit_bytes=mib << 20)
 
-    user_rows, item_rows, user_slopes, item_slopes, count, give, keep = pl.pallas_call(
+    def kernel(function, outs, ins, mib, factor, **more):
+        return pl.pallas_call(
+            function,
+            out_shape=[pltpu.VMEM(shape, dtype) for shape, dtype in outs],
+            out_specs=[vmem] * len(outs),
+            compiler_params=params(mib),
+            cost_estimate=cost(factor),
+            **more,
+        )(*ins)
+
+    user_rows, item_rows, slope, bend, item_vec, item_slopes, count, give, keep = kernel(
         functools.partial(first_kernel, (clients, per, group, shards, head)),
-        out_shape=[
-            pltpu.VMEM((row_count, depth), bf16),
-            pltpu.VMEM((row_count, depth), bf16),
-            pltpu.VMEM((row_count, width), bf16),
-            pltpu.VMEM((row_count, width), bf16),
-            pltpu.VMEM((8, LANES), f32),
-            pltpu.VMEM((quarter, head), f32),
-            pltpu.VMEM((quarter, head), f32),
+        [
+            ((row_count, depth), bf16),
+            ((row_count, depth), bf16),
+            ((row_count, LANES), bf16),
+            ((row_count, width), f32),
+            ((row_count, width), bf16),
+            ((row_count, width), bf16),
+            ((8, LANES), f32),
+            ((quarter, head), f32),
+            ((quarter, head), f32),
         ],
+        in_hbm(picks, ids, user_feats, item_feats, user_weight, item_weight),
+        16,
+        6,
         in_specs=[hbm] * 6,
-        out_specs=[vmem] * 7,
         scratch_shapes=[
             pltpu.SMEM((clients,), i32),
             pltpu.SMEM((clients + 1,), i32),
@@ -333,31 +380,15 @@
             pltpu.VMEM((row_count, LANES), f32),
             pltpu.VMEM((depth, width), bf16),
             pltpu.VMEM((depth, width), bf16),
-            pltpu.VMEM((row_count, width), f32),
-            pltpu.VMEM((row_count, width), bf16),
             pltpu.VMEM((row_count, width), bf16),
             pltpu.SemaphoreType.DMA((2,)),
             pltpu.SemaphoreType.DMA((2,)),
             pltpu.SemaphoreType.DMA((2, clients)),
         ],
-        compiler_params=params(24),
-        cost_estimate=cost(6),
-        name="first",
-    )(*in_hbm(picks, ids, user_feats, item_feats, user_weight, item_weight))
-
-    def terms(flip, skip, after):
-        return pl.pallas_call(
-            functools.partial(terms_kernel, (rows, shards, flip, skip)),
-            out_shape=[
-                pltpu.VMEM((quarter, 2 * width - skip), f32),
-                pltpu.VMEM((quarter, width - skip), f32),
-                pltpu.VMEM((quarter, width), f32),
-            ],
-            in_specs=[vmem] * 5 + [anywhere],
-            out_specs=[vmem] * 3,
-            compiler_params=params(8),
-            cost_estimate=cost(2),
-        )(in_vmem(user_rows), in_vmem(item_rows), in_vmem(user_slopes), in_vmem(item_slopes), in_vmem(count), after)
+    )
+    user_rows, item_rows, slope, bend, item_vec, item_slopes, count = map(
+        in_vmem, (user_rows, item_rows, slope, bend, item_vec, item_slopes, count)
+    )
 
     def swap(value, axis, mask):
         return swapped(value, axis, mask, shards if axis == "client" else clusters)
@@ -365,14 +396,38 @@
     first_sum = swap(give, "client", 1) + keep
     from_first = swap(first_sum, "client", top)
 
-    give, keep_user, keep_item = terms(top, head, count)
-    got = swap(give, "client", 1)
-    second_sum = got[:, : width - head] + keep_user
-    third_sum = got[:, width - head :] + keep_item
+    rest = (quarter, width - head)
+    give, keep = kernel(
+        functools.partial(item_kernel, (rows, shards, head)),
+        [(rest, f32), (rest, f32)],
+        (item_rows, item_slopes, count, first_sum),
+        6,
+        1,
+        in_specs=[vmem] * 3 + [anywhere],
+    )
+    second_sum = swap(give, "client", 1) + keep
     from_second = swap(second_sum, "client", top)
+
+    user_slopes, give, keep = kernel(
+        functools.partial(user_kernel, (per, rows, shards)),
+        [((row_count, width), bf16), ((quarter, width), f32), ((quarter, width), f32)],
+        (user_rows, slope, bend, item_vec, count),
+        6,
+        1,
+        in_specs=[vmem] * 5,
+    )
+    user_slopes = in_vmem(user_slopes)
+    third_sum = swap(give, "client", 1) + keep
     from_third = swap(third_sum, "client", top)
 
-    give, keep_user, keep_item = terms(0, 0, first_sum)
+    give, keep_user, keep_item = kernel(
+        functools.partial(home_kernel, (rows, shards)),
+        [((quarter, 2 * width), f32), ((quarter, width), f32), ((quarter, width), f32)],
+        (user_rows, item_rows, user_slopes, item_slopes, count, second_sum),
+        8,
+        2,
+        in_specs=[vmem] * 5 + [anywhere],
+    )
     got = swap(give, "client", 1)
 
     whole = lambda *shape: pl.BlockSpec(shape, lambda g: (0,) * len(shape))
@@ -403,9 +458,9 @@
         mask *= 2
     loss_table = loss[:clusters, :clients].T
 
-    user_grad = home_user + jnp.concatenate([from_first, from_second], axis=1)
-    from_third, user_grad = lax.optimization_barrier((from_third, user_grad))
-    item_grad = home_item + from_third
+    item_grad = home_item + jnp.concatenate([from_first, from_second], axis=1)
+    from_third, item_grad = lax.optimization_barrier((from_third, item_grad))
+    user_grad = home_user + from_third
     half = shards // 4
     while half > 1:
         half //= 2

time: 69 us -> 69.3 us (level)
  waiting for transfers between devices: 35.5 us -> 37.1 us
  Pallas kernels: 25.8 us -> 24.5 us
    ppermute x9 -> x10, waiting for transfers between devices: 35.5 us -> 37.1 us  [swapped(): return lax.ppermute(value, axis, [(i, i ^ mask) for i in range(size)])]
    pallas_call x3 -> x4, Pallas kernels: 14.2 us -> 12.9 us  [kernel(): pl.pallas_call(function, out_shape=[pltpu.VMEM(shape, dtype) for shape, d...]
    ppermute x9 -> x10, starting transfers between devices: 3.01 us -> 3.02 us  [swapped(): return lax.ppermute(value, axis, [(i, i ^ mask) for i in range(size)])]
  transfers between devices with their start and end apart: 9 -> 10, of which waited for: 5 -> 7; matrix products, arithmetic and copies ran while one was open for 5% -> 4% of each run, Pallas kernels for 24% -> 20%
where the time goes in v2:
time: 69.3 us; the launch traced here: 69.1 us
  waiting for transfers between devices  37.1 us (54%)
  Pallas kernels  24.5 us (35%)
  other arithmetic  3.15 us (5%)
  starting transfers between devices  3.02 us (4%)
  between operations  0.73 us (1%)
    ppermute x10, waiting for transfers between devices, swapped(): return lax.ppermute(value, axis, [(i, i ^ mask) for i in range(size)])  37.1 us
    pallas_call x4, Pallas kernels, kernel(): pl.pallas_call(function, out_shape=[pltpu.VMEM(shape, dtype) for shape, d...  12.9 us
    pallas_call x1, Pallas kernels, body(): pl.pallas_call(functools.partial(loss_kernel, (per, group)), grid=(client...  11.6 us
    ppermute x10, starting transfers between devices, swapped(): return lax.ppermute(value, axis, [(i, i ^ mask) for i in range(size)])  3.02 us
  transfers between devices with their start and end apart: 10, of which 7 were waited for; matrix products, arithmetic and copies ran while one was open for 4% of the time, Pallas kernels for 20%

profile of v2, /device:TPU:30, one launch (start us, length us, event | category | flops | bytes accessed | tf_op | source)
XLA Modules:
  0.0 69.1 jit_solution(9690976096867478943)
XLA Ops:
  0.6 7.2 %shard_map.85 = (bf16[1536,2048]{1,0:T(8,128)(2,1)S(1)}, bf16[1536,2048]{1,0:T(8,128)(2,1)S(1)}, bf16[1536,128]{1,0:T(8,128)(2,1)S(1)}, f32[1536,512]{1,0:T(8,12...) custom-call(s32[16]{0:T(128)} %picks.1, ...), custom_call_target="tpu_custom_call" | custom-call | flops 4831838208 | bytes 1048576 | tf_op jit(solution)/shard_map/pallas_call | solution.py:350
  7.9 0.1 collective-permute-start.1
  8.0 1.5 %collective-permute-done.1 = f32[512,128]{1,0:T(8,128)S(1)} collective-permute-done((f32[512,128]{1,0:T(8,128)S(1)}, f32[512,128]{1,0:T(8,128)S(1)}, u32[]{:S(2)}, u32[]{:S(2)}) %collective-permute-start.1) | collective-permute-done | bytes 262176 | tf_op jit(solution)/shard_map/ppermute | solution.py:311
  9.5 1.2 %shard_map.87 = (f32[512,384]{1,0:T(8,128)S(1)}, f32[512,384]{1,0:T(8,128)S(1)}) custom-call(bf16[1536,2048]{1,0:T(8,128)(2,1)S(1)} %get-tuple-element.32.item_rows, bf16[1536,512]{1,0:T(8,128)(2,1)S(1)} %get-tuple-element.34.item_slopes, f32[8,128]{1,0:T(8,128)S(1)} %get-tuple-element.29.count_v, f32[512,128]{1,0:T(8,128)S(1)} %add.31.after), custom_call_target="tpu_custom_call" | custom-call | flops 805306368 | bytes 1048576 | tf_op jit(solution)/shard_map/pallas_call | solution.py:350
  10.7 0.2 collective-permute-start.2
  10.9 1.9 %shard_map.86 = (bf16[1536,512]{1,0:T(8,128)(2,1)S(1)}, f32[512,512]{1,0:T(8,128)S(1)}, f32[512,512]{1,0:T(8,128)S(1)}) custom-call(bf16[1536,2048]{1,0:T(8,128)(2,1)S(1)} %get-tuple-element.25.user_rows, bf16[1536,128]{1,0:T(8,128)(2,1)S(1)} %get-tuple-element.26.slope_v, f32[1536,512]{1,0:T(8,128)S(1)} %get-tuple-element.27.bend_v, ...), custom_call_target="tpu_custom_call" | custom-call | flops 805306368 | bytes 1048576 | tf_op jit(solution)/shard_map/pallas_call | solution.py:350
  12.7 0.3 collective-permute-done.2
  13.0 0.1 add.32.after
  13.1 2.6 %shard_map.88 = (f32[512,1024]{1,0:T(8,128)S(1)}, f32[512,512]{1,0:T(8,128)S(1)}, f32[512,512]{1,0:T(8,128)S(1)}) custom-call(bf16[1536,2048]{1,0:T(8,128)(2,1)S(1)} %get-tuple-element.25.user_rows, bf16[1536,2048]{1,0:T(8,128)(2,1)S(1)} %get-tuple-element.32.item_rows, bf16[1536,512]{1,0:T(8,128)(2,1)S(1)} %get-tuple-element.33.user_slopes, ...), custom_call_target="tpu_custom_call" | custom-call | flops 1610612736 | bytes 1048576 | tf_op jit(solution)/shard_map/pallas_call | solution.py:350
  15.8 0.2 collective-permute-start.3
  16.0 0.4 collective-permute-start
  16.3 0.0 collective-permute-start.8
  16.3 2.0 %collective-permute-start.9 = (f32[512,384]{1,0:T(8,128)S(1)}, f32[512,384]{1,0:T(8,128)S(1)}, u32[]{:S(2)}, u32[]{:S(2)}) collective-permute-start(f32[512,384]{1,0:T(8,128)S(1)} %add.32.after), channel_id=1, source_target_pairs={{0,2},{1,3},{2,0},{3,1},{4,6},{5,7},{6,4},{7,5},{8,10},{9,11},{10,... | collective-permute-start | bytes 2359304 | tf_op jit(solution)/shard_map/ppermute | solution.py:311
  18.4 3.1 %collective-permute-done = f32[512,512]{1,0:T(8,128)S(1)} collective-permute-done((f32[512,512]{1,0:T(8,128)S(1)}, f32[512,512]{1,0:T(8,128)S(1)}, u32[]{:S(2)}, u32[]{:S(2)}) %collective-permute-start) | collective-permute-done | bytes 1048608 | tf_op jit(solution)/shard_map/ppermute | solution.py:311
  21.5 0.2 add.30.after
  21.7 0.1 collective-permute-start.7
  21.8 11.6 %loss.1 = f32[8,128]{1,0:T(8,128)S(1)} custom-call(s32[12,128]{1,0:T(8,128)} %bitcast.8, bf16[1536,2048]{1,0:T(8,128)(2,1)} %user_feats.3, bf16[1536,2048]{1,0:T(8,128)(2,1)} %item_feats.3, bf16[1,2048,512]{2,1,0:T(8,128)(2,1)} %user_weight.3, bf16[1,2048,512]{2,1,0:T(8,128)(2,1)} %item_weight.3, f32[512,512]{1,0:T(8,128)S(1)} %add.30.after), custom_call_target="tpu_custom_call" | custom-call | flops 6442450944 | bytes 1048576 | tf_op jit(solution)/shard_map/loss/pallas_call | solution.py:434
  33.4 0.0 collective-permute-done.3
  33.4 0.5 slice_add_fusion
  33.9 0.1 collective-permute-start.4
  34.0 3.6 %collective-permute-done.4 = f32[8,128]{1,0:T(8,128)S(1)} collective-permute-done((f32[8,128]{1,0:T(8,128)S(1)}, f32[8,128]{1,0:T(8,128)S(1)}, u32[]{:S(2)}, u32[]{:S(2)}) %collective-permute-start.4) | collective-permute-done | bytes 4128 | tf_op jit(solution)/shard_map/ppermute | solution.py:311
  37.6 0.0 collective-permute-start.5
  37.6 0.0 collective-permute-done.8
  37.6 4.8 %collective-permute-done.9 = f32[512,384]{1,0:T(8,128)S(1)} collective-permute-done((f32[512,384]{1,0:T(8,128)S(1)}, f32[512,384]{1,0:T(8,128)S(1)}, u32[]{:S(2)}, u32[]{:S(2)}) %collective-permute-start.9) | collective-permute-done | bytes 786464 | tf_op jit(solution)/shard_map/ppermute | solution.py:311
  42.4 1.1 %maximum_add_fusion = f32[512,512]{1,0:T(8,128)} fusion(f32[512,512]{1,0:T(8,128)S(1)} %get-tuple-element.44, f32[512,384]{1,0:T(8,128)S(1)} %collective-permute-done.9, f32[512,128]{1,0:T(8,128)S(1)} %collective-permute-done.8), kind=kLoop, calls=%fused_computation.2 | loop fusion | flops 524288 | bytes 3145728 | tf_op jit(solution)/shard_map/add | solution.py:461
  43.5 20.5 %collective-permute-done.7 = f32[512,512]{1,0:T(8,128)S(1)} collective-permute-done((f32[512,512]{1,0:T(8,128)S(1)}, f32[512,512]{1,0:T(8,128)S(1)}, u32[]{:S(2)}, u32[]{:S(2)}) %collective-permute-start.7) | collective-permute-done | bytes 1048608 | tf_op jit(solution)/shard_map/ppermute | solution.py:311
  64.0 0.0 collective-permute-done.5
  64.0 0.0 collective-permute-start.6
  64.0 1.2 %add_bitcast_fusion = f32[1,512,512]{2,1,0:T(8,128)} fusion(f32[512,512]{1,0:T(8,128)S(1)} %get-tuple-element.43, f32[512,512]{1,0:T(8,128)S(1)} %collective-permute-done.7), kind=kLoop, calls=%fused_computation.3 | loop fusion | flops 262144 | bytes 3145728 | tf_op jit(solution)/shard_map/broadcast_in_dim | solution.py:471
  65.2 3.3 %collective-permute-done.6 = f32[8,128]{1,0:T(8,128)S(1)} collective-permute-done((f32[8,128]{1,0:T(8,128)S(1)}, f32[8,128]{1,0:T(8,128)S(1)}, u32[]{:S(2)}, u32[]{:S(2)}) %collective-permute-start.6) | collective-permute-done | bytes 4128 | tf_op jit(solution)/shard_map/ppermute | solution.py:311
  68.5 0.6 slice_bitcast_fusion
  (4 shorter events, 0.0 us)
Async XLA Ops:
  7.9 1.6 %collective-permute-start.1 = (f32[512,128]{1,0:T(8,128)S(1)}, f32[512,128]{1,0:T(8,128)S(1)}, u32[]{:S(2)}, u32[]{:S(2)}) collective-permute-start(f32[512,128]{1,0:T(8,128)S(1)} %get-tuple-element.35), channel_id=1, source_target_pairs={{0,1},{1,0},{2,3},{3,2},{4,5},{5,4},{6,7},{7,6},{8,9},{9,8},{10,11... | collective-permute-start | bytes 786440 | tf_op jit(solution)/shard_map/ppermute | solution.py:311
  10.7 2.4 %collective-permute-start.2 = (f32[512,384]{1,0:T(8,128)S(1)}, f32[512,384]{1,0:T(8,128)S(1)}, u32[]{:S(2)}, u32[]{:S(2)}) collective-permute-start(f32[512,384]{1,0:T(8,128)S(1)} %get-tuple-element.37), channel_id=1, source_target_pairs={{0,1},{1,0},{2,3},{3,2},{4,5},{5,4},{6,7},{7,6},{8,9},{9,8},{10,11... | collective-permute-start | bytes 2359304 | tf_op jit(solution)/shard_map/ppermute | solution.py:311
  15.8 17.7 %collective-permute-start.3 = (f32[512,1024]{1,0:T(8,128)S(1)}, f32[512,1024]{1,0:T(8,128)S(1)}, u32[]{:S(2)}, u32[]{:S(2)}) collective-permute-start(f32[512,1024]{1,0:T(8,128)S(1)} %get-tuple-element.39), channel_id=1, source_target_pairs={{0,1},{1,0},{2,3},{3,2},{4,5},{5,4},{6,7},{7,6},{8,9},{9,8},{10,11... | collective-permute-start | bytes 6291464 | tf_op jit(solution)/shard_map/ppermute | solution.py:311
  16.0 5.5 %collective-permute-start = (f32[512,512]{1,0:T(8,128)S(1)}, f32[512,512]{1,0:T(8,128)S(1)}, u32[]{:S(2)}, u32[]{:S(2)}) collective-permute-start(f32[512,512]{1,0:T(8,128)S(1)} %get-tuple-element.30), channel_id=1, source_target_pairs={{0,1},{1,0},{2,3},{3,2},{4,5},{5,4},{6,7},{7,6},{8,9},{9,8},{10,11... | collective-permute-start | bytes 3145736 | tf_op jit(solution)/shard_map/ppermute | solution.py:311
  16.3 21.3 %collective-permute-start.8 = (f32[512,128]{1,0:T(8,128)S(1)}, f32[512,128]{1,0:T(8,128)S(1)}, u32[]{:S(2)}, u32[]{:S(2)}) collective-permute-start(f32[512,128]{1,0:T(8,128)S(1)} %add.31.after), channel_id=1, source_target_pairs={{0,2},{1,3},{2,0},{3,1},{4,6},{5,7},{6,4},{7,5},{8,10},{9,11},{10,... | collective-permute-start | bytes 786440 | tf_op jit(solution)/shard_map/ppermute | solution.py:311
  16.3 26.0 %collective-permute-start.9 = (f32[512,384]{1,0:T(8,128)S(1)}, f32[512,384]{1,0:T(8,128)S(1)}, u32[]{:S(2)}, u32[]{:S(2)}) collective-permute-start(f32[512,384]{1,0:T(8,128)S(1)} %add.32.after), channel_id=1, source_target_pairs={{0,2},{1,3},{2,0},{3,1},{4,6},{5,7},{6,4},{7,5},{8,10},{9,11},{10,... | collective-permute-start | bytes 2359304 | tf_op jit(solution)/shard_map/ppermute | solution.py:311
  21.7 42.3 %collective-permute-start.7 = (f32[512,512]{1,0:T(8,128)S(1)}, f32[512,512]{1,0:T(8,128)S(1)}, u32[]{:S(2)}, u32[]{:S(2)}) collective-permute-start(f32[512,512]{1,0:T(8,128)S(1)} %add.30.after), channel_id=1, source_target_pairs={{0,2},{1,3},{2,0},{3,1},{4,6},{5,7},{6,4},{7,5},{8,10},{9,11},{10,... | collective-permute-start | bytes 3145736 | tf_op jit(solution)/shard_map/ppermute | solution.py:311
  33.9 3.7 %collective-permute-start.4 = (f32[8,128]{1,0:T(8,128)S(1)}, f32[8,128]{1,0:T(8,128)S(1)}, u32[]{:S(2)}, u32[]{:S(2)}) collective-permute-start(f32[8,128]{1,0:T(8,128)S(1)} %loss.1), channel_id=1, source_target_pairs={{0,4},{4,0},{8,12},{12,8},{16,20},{20,16},{24,28},{28,24},{1,5},{5... | collective-permute-start | bytes 12296 | tf_op jit(solution)/shard_map/ppermute | solution.py:311
  37.6 26.4 %collective-permute-start.5 = (f32[8,128]{1,0:T(8,128)S(1)}, f32[8,128]{1,0:T(8,128)S(1)}, u32[]{:S(2)}, u32[]{:S(2)}) collective-permute-start(f32[8,128]{1,0:T(8,128)S(1)} %add.35), channel_id=1, source_target_pairs={{0,8},{4,12},{8,0},{12,4},{16,24},{20,28},{24,16},{28,20},{1,9},{5... | collective-permute-start | bytes 12296 | tf_op jit(solution)/shard_map/ppermute | solution.py:311
  64.0 4.5 %collective-permute-start.6 = (f32[8,128]{1,0:T(8,128)S(1)}, f32[8,128]{1,0:T(8,128)S(1)}, u32[]{:S(2)}, u32[]{:S(2)}) collective-permute-start(f32[8,128]{1,0:T(8,128)S(1)} %add.36), channel_id=1, source_target_pairs={{0,16},{4,20},{8,24},{12,28},{16,0},{20,4},{24,8},{28,12},{1,17},{... | collective-permute-start | bytes 12296 | tf_op jit(solution)/shard_map/ppermute | solution.py:311

commit v3 on v2

--- a/solution.py
+++ b/solution.py
@@ -305,6 +305,15 @@
         loss = jnp.sum(jnp.sum(pair, axis=1, keepdims=True), axis=0, keepdims=True) / (per * per)
         losses = jnp.where((row == mine) & (lane == client), loss, losses)
     loss_v[...] = losses
+
+
+def finish_kernel(start, home, piece, *refs):
+    out, total, sem = refs[-3:]
+    cols = slice(start, start + piece.shape[1])
+    total[...] = home[:, cols] + piece[...]
+    copy = pltpu.make_async_copy(total, out.at[:, cols], sem.at[0])
+    copy.start()
+    copy.wait()
 
 
 def swapped(value, axis, mask, size):
@@ -418,7 +427,8 @@
     )
     user_slopes = in_vmem(user_slopes)
     third_sum = swap(give, "client", 1) + keep
-    from_third = swap(third_sum, "client", top)
+    from_third = swap(third_sum[:, head:], "client", top)
+    from_fourth = swap(third_sum[:, :head], "client", top)
 
     give, keep_user, keep_item = kernel(
         functools.partial(home_kernel, (rows, shards)),
@@ -460,7 +470,22 @@
 
     item_grad = home_item + jnp.concatenate([from_first, from_second], axis=1)
     from_third, item_grad = lax.optimization_barrier((from_third, item_grad))
-    user_grad = home_user + from_third
+
+    def finish(piece, start, *so_far):
+        return pl.pallas_call(
+            functools.partial(finish_kernel, start),
+            out_shape=pltpu.HBM(home_user.shape, f32),
+            in_specs=[vmem, vmem] + [hbm] * len(so_far),
+            out_specs=hbm,
+            scratch_shapes=[pltpu.VMEM(piece.shape, f32), pltpu.SemaphoreType.DMA((1,))],
+            input_output_aliases={2: 0} if so_far else {},
+            compiler_params=params(4),
+            name="finish",
+        )(in_vmem(home_user), in_vmem(piece), *so_far)
+
+    most = finish(from_third, head)
+    most, from_fourth = lax.optimization_barrier((most, from_fourth))
+    user_grad = finish(from_fourth, 0, *in_hbm(most))
     half = shards // 4
     while half > 1:
         half //= 2

time: 69.3 us -> 65.6 us (0.947)
  waiting for transfers between devices: 37.1 us -> 30.6 us
  starting transfers between devices: 3.02 us -> 5.08 us
  Pallas kernels: 24.5 us -> 26.3 us
  other arithmetic: 3.15 us -> 1.98 us
    ppermute x10 -> x11, waiting for transfers between devices: 37.1 us -> 30.6 us  [swapped(): return lax.ppermute(value, axis, [(i, i ^ mask) for i in range(size)])]
    ppermute x10 -> x11, starting transfers between devices: 3.02 us -> 5.08 us  [swapped(): return lax.ppermute(value, axis, [(i, i ^ mask) for i in range(size)])]
    pallas_call x0 -> x2, Pallas kernels: none -> 1.78 us  [finish(): pl.pallas_call(functools.partial(finish_kernel, start), out_shape=pltpu.H...]
    broadcast_in_dim x1 -> x0, other arithmetic: 1.18 us -> none  [body(): return (loss_table, user_grad[None], item_grad[None])]
  transfers between devices with their start and end apart: 10 -> 11, of which waited for: 7 -> 8; matrix products, arithmetic and copies ran while one was open for 4% -> 3% of each run, Pallas kernels for 20% -> 23%
where the time goes in v3:
time: 65.6 us; the launch traced here: 65.4 us
  waiting for transfers between devices  30.6 us (47%)
  Pallas kernels  26.3 us (40%)
  starting transfers between devices  5.08 us (8%)
  other arithmetic  1.98 us (3%)
  between operations  0.77 us (1%)
  local copies, waits for them, and re-layouts  0.7 us (1%)
    ppermute x11, waiting for transfers between devices, swapped(): return lax.ppermute(value, axis, [(i, i ^ mask) for i in range(size)])  30.6 us
    pallas_call x4, Pallas kernels, kernel(): pl.pallas_call(function, out_shape=[pltpu.VMEM(shape, dtype) for shape, d...  12.9 us
    pallas_call x1, Pallas kernels, body(): pl.pallas_call(functools.partial(loss_kernel, (per, group)), grid=(client...  11.6 us
    ppermute x11, starting transfers between devices, swapped(): return lax.ppermute(value, axis, [(i, i ^ mask) for i in range(size)])  5.08 us
    pallas_call x2, Pallas kernels, finish(): pl.pallas_call(functools.partial(finish_kernel, start), out_shape=pltpu.H...  1.78 us
  transfers between devices with their start and end apart: 11, of which 8 were waited for; matrix products, arithmetic and copies ran while one was open for 3% of the time, Pallas kernels for 23%

profile of v3, /device:TPU:30, one launch (start us, length us, event | category | flops | bytes accessed | tf_op | source)
XLA Modules:
  0.0 65.4 jit_solution(11736579733646757383)
XLA Ops:
  0.6 7.2 %shard_map.85 = (bf16[1536,2048]{1,0:T(8,128)(2,1)S(1)}, bf16[1536,2048]{1,0:T(8,128)(2,1)S(1)}, bf16[1536,128]{1,0:T(8,128)(2,1)S(1)}, f32[1536,512]{1,0:T(8,12...) custom-call(s32[16]{0:T(128)} %picks.1, ...), custom_call_target="tpu_custom_call" | custom-call | flops 4831838208 | bytes 1048576 | tf_op jit(solution)/shard_map/pallas_call | solution.py:359
  7.9 0.1 collective-permute-start.1
  8.0 1.5 %collective-permute-done.1 = f32[512,128]{1,0:T(8,128)S(1)} collective-permute-done((f32[512,128]{1,0:T(8,128)S(1)}, f32[512,128]{1,0:T(8,128)S(1)}, u32[]{:S(2)}, u32[]{:S(2)}) %collective-permute-start.1) | collective-permute-done | bytes 262176 | tf_op jit(solution)/shard_map/ppermute | solution.py:320
  9.5 1.2 %shard_map.87 = (f32[512,384]{1,0:T(8,128)S(1)}, f32[512,384]{1,0:T(8,128)S(1)}) custom-call(bf16[1536,2048]{1,0:T(8,128)(2,1)S(1)} %get-tuple-element.34.item_rows, bf16[1536,512]{1,0:T(8,128)(2,1)S(1)} %get-tuple-element.36.item_slopes, f32[8,128]{1,0:T(8,128)S(1)} %get-tuple-element.31.count_v, f32[512,128]{1,0:T(8,128)S(1)} %add.28.after), custom_call_target="tpu_custom_call" | custom-call | flops 805306368 | bytes 1048576 | tf_op jit(solution)/shard_map/pallas_call | solution.py:359
  10.7 0.2 collective-permute-start.2
  10.9 1.9 %shard_map.86 = (bf16[1536,512]{1,0:T(8,128)(2,1)S(1)}, f32[512,512]{1,0:T(8,128)S(1)}, f32[512,512]{1,0:T(8,128)S(1)}) custom-call(bf16[1536,2048]{1,0:T(8,128)(2,1)S(1)} %get-tuple-element.27.user_rows, bf16[1536,128]{1,0:T(8,128)(2,1)S(1)} %get-tuple-element.28.slope_v, f32[1536,512]{1,0:T(8,128)S(1)} %get-tuple-element.29.bend_v, ...), custom_call_target="tpu_custom_call" | custom-call | flops 805306368 | bytes 1048576 | tf_op jit(solution)/shard_map/pallas_call | solution.py:359
  12.7 0.3 collective-permute-done.2
  13.0 0.1 add.29.after
  13.1 2.6 %shard_map.88 = (f32[512,1024]{1,0:T(8,128)S(1)}, f32[512,512]{1,0:T(8,128)S(1)}, f32[512,512]{1,0:T(8,128)S(1)}) custom-call(bf16[1536,2048]{1,0:T(8,128)(2,1)S(1)} %get-tuple-element.27.user_rows, bf16[1536,2048]{1,0:T(8,128)(2,1)S(1)} %get-tuple-element.34.item_rows, bf16[1536,512]{1,0:T(8,128)(2,1)S(1)} %get-tuple-element.35.user_slopes, ...), custom_call_target="tpu_custom_call" | custom-call | flops 1610612736 | bytes 1048576 | tf_op jit(solution)/shard_map/pallas_call | solution.py:359
  15.8 0.2 collective-permute-start.3
  16.0 0.4 collective-permute-start
  16.3 0.0 collective-permute-start.8
  16.3 2.0 %collective-permute-start.9 = (f32[512,384]{1,0:T(8,128)S(1)}, f32[512,384]{1,0:T(8,128)S(1)}, u32[]{:S(2)}, u32[]{:S(2)}) collective-permute-start(f32[512,384]{1,0:T(8,128)S(1)} %add.29.after), channel_id=1, source_target_pairs={{0,2},{1,3},{2,0},{3,1},{4,6},{5,7},{6,4},{7,5},{8,10},{9,11},{10,... | collective-permute-start | bytes 2359304 | tf_op jit(solution)/shard_map/ppermute | solution.py:320
  18.4 3.1 %collective-permute-done = f32[512,512]{1,0:T(8,128)S(1)} collective-permute-done((f32[512,512]{1,0:T(8,128)S(1)}, f32[512,512]{1,0:T(8,128)S(1)}, u32[]{:S(2)}, u32[]{:S(2)}) %collective-permute-start) | collective-permute-done | bytes 1048608 | tf_op jit(solution)/shard_map/ppermute | solution.py:320
  21.5 0.2 add.27.after
  21.7 0.1 slice.22
  21.8 0.1 collective-permute-start.7
  21.9 11.6 %loss.1 = f32[8,128]{1,0:T(8,128)S(1)} custom-call(s32[12,128]{1,0:T(8,128)} %bitcast.8, bf16[1536,2048]{1,0:T(8,128)(2,1)} %user_feats.3, bf16[1536,2048]{1,0:T(8,128)(2,1)} %item_feats.3, bf16[1,2048,512]{2,1,0:T(8,128)(2,1)} %user_weight.3, bf16[1,2048,512]{2,1,0:T(8,128)(2,1)} %item_weight.3, f32[512,512]{1,0:T(8,128)S(1)} %add.27.after), custom_call_target="tpu_custom_call" | custom-call | flops 6442450944 | bytes 1048576 | tf_op jit(solution)/shard_map/loss/pallas_call | solution.py:444
  33.5 0.0 collective-permute-done.3
  33.5 0.5 slice_add_fusion
  34.0 0.1 collective-permute-start.4
  34.1 3.6 %collective-permute-done.4 = f32[8,128]{1,0:T(8,128)S(1)} collective-permute-done((f32[8,128]{1,0:T(8,128)S(1)}, f32[8,128]{1,0:T(8,128)S(1)}, u32[]{:S(2)}, u32[]{:S(2)}) %collective-permute-start.4) | collective-permute-done | bytes 4128 | tf_op jit(solution)/shard_map/ppermute | solution.py:320
  37.7 0.0 collective-permute-start.5
  37.7 2.1 %collective-permute-start.10 = (f32[512,128]{1,0:T(8,128)S(1)}, f32[512,128]{1,0:T(8,128)S(1)}, u32[]{:S(2)}, u32[]{:S(2)}) collective-permute-start(f32[512,128]{1,0:T(8,128)S(1)} %slice.23), channel_id=1, source_target_pairs={{0,2},{1,3},{2,0},{3,1},{4,6},{5,7},{6,4},{7,5},{8,10},{9,11},{10,... | collective-permute-start | bytes 786440 | tf_op jit(solution)/shard_map/ppermute | solution.py:320
  39.8 1.5 %collective-permute-done.5 = f32[8,128]{1,0:T(8,128)S(1)} collective-permute-done((f32[8,128]{1,0:T(8,128)S(1)}, f32[8,128]{1,0:T(8,128)S(1)}, u32[]{:S(2)}, u32[]{:S(2)}) %collective-permute-start.5) | collective-permute-done | bytes 4128 | tf_op jit(solution)/shard_map/ppermute | solution.py:320
  41.3 0.0 collective-permute-start.6
  41.3 0.0 collective-permute-done.8
  41.3 1.1 %collective-permute-done.9 = f32[512,384]{1,0:T(8,128)S(1)} collective-permute-done((f32[512,384]{1,0:T(8,128)S(1)}, f32[512,384]{1,0:T(8,128)S(1)}, u32[]{:S(2)}, u32[]{:S(2)}) %collective-permute-start.9) | collective-permute-done | bytes 786464 | tf_op jit(solution)/shard_map/ppermute | solution.py:320
  42.4 1.1 %maximum_add_fusion = f32[512,512]{1,0:T(8,128)} fusion(f32[512,512]{1,0:T(8,128)S(1)} %get-tuple-element.46, f32[512,384]{1,0:T(8,128)S(1)} %collective-permute-done.9, f32[512,128]{1,0:T(8,128)S(1)} %collective-permute-done.8), kind=kLoop, calls=%fused_computation.2 | loop fusion | flops 524288 | bytes 3145728 | tf_op jit(solution)/shard_map/add | solution.py:471
  43.5 15.7 %collective-permute-done.7.piece = f32[512,384]{1,0:T(8,128)S(1)} collective-permute-done((f32[512,384]{1,0:T(8,128)S(1)}, f32[512,384]{1,0:T(8,128)S(1)}, u32[]{:S(2)}, u32[]{:S(2)}) %collective-permute-start.7) | collective-permute-done | bytes 786464 | tf_op jit(solution)/shard_map/ppermute | solution.py:320
  59.2 1.0 %finish.2.refs_0_ = f32[512,512]{1,0:T(8,128)} custom-call(f32[512,512]{1,0:T(8,128)S(1)} %get-tuple-element.45.home, f32[512,384]{1,0:T(8,128)S(1)} %collective-permute-done.7.piece), custom_call_target="tpu_custom_call" | custom-call | tf_op jit(solution)/shard_map/finish/pallas_call | solution.py:475
  60.2 3.8 %collective-permute-done.10.piece = f32[512,128]{1,0:T(8,128)S(1)} collective-permute-done((f32[512,128]{1,0:T(8,128)S(1)}, f32[512,128]{1,0:T(8,128)S(1)}, u32[]{:S(2)}, u32[]{:S(2)}) %collective-permute-start.10) | collective-permute-done | bytes 262176 | tf_op jit(solution)/shard_map/ppermute | solution.py:320
  64.0 0.8 %finish.3 = f32[512,512]{1,0:T(8,128)} custom-call(f32[512,512]{1,0:T(8,128)S(1)} %get-tuple-element.45.home, f32[512,128]{1,0:T(8,128)S(1)} %collective-permute-done.10.piece, f32[512,512]{1,0:T(8,128)} %finish.2.refs_0_), custom_call_target="tpu_custom_call", output_to_operand_aliasing={{}: (2, {})} | custom-call | tf_op jit(solution)/shard_map/finish/pallas_call | solution.py:475
  64.8 0.0 collective-permute-done.6
  64.8 0.6 slice_bitcast_fusion
  (5 shorter events, 0.1 us)
Async XLA Ops:
  7.9 1.6 %collective-permute-start.1 = (f32[512,128]{1,0:T(8,128)S(1)}, f32[512,128]{1,0:T(8,128)S(1)}, u32[]{:S(2)}, u32[]{:S(2)}) collective-permute-start(f32[512,128]{1,0:T(8,128)S(1)} %get-tuple-element.37), channel_id=1, source_target_pairs={{0,1},{1,0},{2,3},{3,2},{4,5},{5,4},{6,7},{7,6},{8,9},{9,8},{10,11... | collective-permute-start | bytes 786440 | tf_op jit(solution)/shard_map/ppermute | solution.py:320
  10.7 2.4 %collective-permute-start.2 = (f32[512,384]{1,0:T(8,128)S(1)}, f32[512,384]{1,0:T(8,128)S(1)}, u32[]{:S(2)}, u32[]{:S(2)}) collective-permute-start(f32[512,384]{1,0:T(8,128)S(1)} %get-tuple-element.39), channel_id=1, source_target_pairs={{0,1},{1,0},{2,3},{3,2},{4,5},{5,4},{6,7},{7,6},{8,9},{9,8},{10,11... | collective-permute-start | bytes 2359304 | tf_op jit(solution)/shard_map/ppermute | solution.py:320
  15.8 17.7 %collective-permute-start.3 = (f32[512,1024]{1,0:T(8,128)S(1)}, f32[512,1024]{1,0:T(8,128)S(1)}, u32[]{:S(2)}, u32[]{:S(2)}) collective-permute-start(f32[512,1024]{1,0:T(8,128)S(1)} %get-tuple-element.41), channel_id=1, source_target_pairs={{0,1},{1,0},{2,3},{3,2},{4,5},{5,4},{6,7},{7,6},{8,9},{9,8},{10,11... | collective-permute-start | bytes 6291464 | tf_op jit(solution)/shard_map/ppermute | solution.py:320
  16.0 5.5 %collective-permute-start = (f32[512,512]{1,0:T(8,128)S(1)}, f32[512,512]{1,0:T(8,128)S(1)}, u32[]{:S(2)}, u32[]{:S(2)}) collective-permute-start(f32[512,512]{1,0:T(8,128)S(1)} %get-tuple-element.32), channel_id=1, source_target_pairs={{0,1},{1,0},{2,3},{3,2},{4,5},{5,4},{6,7},{7,6},{8,9},{9,8},{10,11... | collective-permute-start | bytes 3145736 | tf_op jit(solution)/shard_map/ppermute | solution.py:320
  16.3 25.0 %collective-permute-start.8 = (f32[512,128]{1,0:T(8,128)S(1)}, f32[512,128]{1,0:T(8,128)S(1)}, u32[]{:S(2)}, u32[]{:S(2)}) collective-permute-start(f32[512,128]{1,0:T(8,128)S(1)} %add.28.after), channel_id=1, source_target_pairs={{0,2},{1,3},{2,0},{3,1},{4,6},{5,7},{6,4},{7,5},{8,10},{9,11},{10,... | collective-permute-start | bytes 786440 | tf_op jit(solution)/shard_map/ppermute | solution.py:320
  16.3 26.0 %collective-permute-start.9 = (f32[512,384]{1,0:T(8,128)S(1)}, f32[512,384]{1,0:T(8,128)S(1)}, u32[]{:S(2)}, u32[]{:S(2)}) collective-permute-start(f32[512,384]{1,0:T(8,128)S(1)} %add.29.after), channel_id=1, source_target_pairs={{0,2},{1,3},{2,0},{3,1},{4,6},{5,7},{6,4},{7,5},{8,10},{9,11},{10,... | collective-permute-start | bytes 2359304 | tf_op jit(solution)/shard_map/ppermute | solution.py:320
  21.8 37.4 %collective-permute-start.7 = (f32[512,384]{1,0:T(8,128)S(1)}, f32[512,384]{1,0:T(8,128)S(1)}, u32[]{:S(2)}, u32[]{:S(2)}) collective-permute-start(f32[512,384]{1,0:T(8,128)S(1)} %slice.22), channel_id=1, source_target_pairs={{0,2},{1,3},{2,0},{3,1},{4,6},{5,7},{6,4},{7,5},{8,10},{9,11},{10,... | collective-permute-start | bytes 2359304 | tf_op jit(solution)/shard_map/ppermute | solution.py:320
  34.0 3.7 %collective-permute-start.4 = (f32[8,128]{1,0:T(8,128)S(1)}, f32[8,128]{1,0:T(8,128)S(1)}, u32[]{:S(2)}, u32[]{:S(2)}) collective-permute-start(f32[8,128]{1,0:T(8,128)S(1)} %loss.1), channel_id=1, source_target_pairs={{0,4},{4,0},{8,12},{12,8},{16,20},{20,16},{24,28},{28,24},{1,5},{5... | collective-permute-start | bytes 12296 | tf_op jit(solution)/shard_map/ppermute | solution.py:320
  37.7 3.6 %collective-permute-start.5 = (f32[8,128]{1,0:T(8,128)S(1)}, f32[8,128]{1,0:T(8,128)S(1)}, u32[]{:S(2)}, u32[]{:S(2)}) collective-permute-start(f32[8,128]{1,0:T(8,128)S(1)} %add.32), channel_id=1, source_target_pairs={{0,8},{4,12},{8,0},{12,4},{16,24},{20,28},{24,16},{28,20},{1,9},{5... | collective-permute-start | bytes 12296 | tf_op jit(solution)/shard_map/ppermute | solution.py:320
  37.7 26.3 %collective-permute-start.10 = (f32[512,128]{1,0:T(8,128)S(1)}, f32[512,128]{1,0:T(8,128)S(1)}, u32[]{:S(2)}, u32[]{:S(2)}) collective-permute-start(f32[512,128]{1,0:T(8,128)S(1)} %slice.23), channel_id=1, source_target_pairs={{0,2},{1,3},{2,0},{3,1},{4,6},{5,7},{6,4},{7,5},{8,10},{9,11},{10,... | collective-permute-start | bytes 786440 | tf_op jit(solution)/shard_map/ppermute | solution.py:320
  41.3 23.5 %collective-permute-start.6 = (f32[8,128]{1,0:T(8,128)S(1)}, f32[8,128]{1,0:T(8,128)S(1)}, u32[]{:S(2)}, u32[]{:S(2)}) collective-permute-start(f32[8,128]{1,0:T(8,128)S(1)} %add.33), channel_id=1, source_target_pairs={{0,16},{4,20},{8,24},{12,28},{16,0},{20,4},{24,8},{28,12},{1,17},{... | collective-permute-start | bytes 12296 | tf_op jit(solution)/shard_map/ppermute | solution.py:320
